TPU v7x, 8 devices: a whole 2x2x1 slice. The times are simulated.
8 devices in a mesh: model: 4 (over z, y, x), data: 2 (over core).
Axes of the slice: x: 2, y: 2, z: 1, core: 2. Of those that a mesh axis runs over, the one named last changes fastest.
Arguments:
- x_tokens: bfloat16 [8192, 3072], P('data')
- dy_tokens: bfloat16 [8192, 3072], P('data')
- w_col: bfloat16 [2, 3072, 3072], P(None, None, 'model')
- w_row: bfloat16 [2, 3072, 3072], P(None, 'model')
- a_old_col: float32 [2, 3072, 3072], replicated
- s_old_col: float32 [2, 3072, 768], P(None, 'model')
- a_old_row: float32 [2, 3072, 768], P(None, 'model')
- s_old_row: float32 [2, 3072, 3072], replicated
- a_inv_col: float32 [2, 3072, 3072], replicated
- s_inv_col: float32 [2, 3072, 768], P(None, 'model')
- a_inv_row: float32 [2, 3072, 768], P(None, 'model')
- s_inv_row: float32 [2, 3072, 3072], replicated
Outputs:
- output 1: float32 [2, 3072, 3072], P(None, None, 'model')
- output 2: float32 [2, 3072, 3072], P(None, 'model')
- output 3: float32 [2, 3072, 3072], replicated
- output 4: float32 [2, 3072, 768], P(None, 'model')
- output 5: float32 [2, 3072, 768], P(None, 'model')
- output 6: float32 [2, 3072, 3072], replicated
All inputs are finite; a program needn't handle non-finite values.
Results may differ from a plain program's by a relative error of at most 0.00613152.
Values are sent between devices in bfloat16 or wider.
A program may use at most 2.25 GiB of HBM per device.

v0:
```python
import math
import jax
import jax.numpy as jnp
from jax import lax
from jax.sharding import PartitionSpec as P

FACTOR_DECAY = 0.8
GELU_SCALE = math.sqrt(2.0 / math.pi)
GELU_CUBIC = 0.044715
EXACT = lax.Precision.HIGHEST
TN_DIMS = (((0,), (0,)), ((), ()))
NT_DIMS = (((1,), (1,)), ((), ()))


def gelu_value(pre_act):
    tanh_arg = GELU_SCALE * (pre_act + GELU_CUBIC * pre_act * pre_act * pre_act)
    return 0.5 * pre_act * (1.0 + jnp.tanh(tanh_arg))


def gelu_slope(pre_act):
    tanh_arg = GELU_SCALE * (pre_act + GELU_CUBIC * pre_act * pre_act * pre_act)
    tanh_val = jnp.tanh(tanh_arg)
    return 0.5 * (1.0 + tanh_val) + 0.5 * pre_act * (1.0 - tanh_val * tanh_val) * GELU_SCALE * (1.0 + 3.0 * GELU_CUBIC * pre_act * pre_act)


def activate(pre_act):
    return gelu_value(pre_act.astype(jnp.float32)).astype(jnp.bfloat16)


def back_gate(grad_act, pre_act):
    return (grad_act.astype(jnp.float32) * gelu_slope(pre_act.astype(jnp.float32))).astype(jnp.bfloat16)


def matmul(left_mat, right_mat):
    return jnp.dot(left_mat, right_mat, preferred_element_type=jnp.float32)


def matmul_tn(left_mat, right_mat):
    return lax.dot_general(left_mat, right_mat, TN_DIMS, preferred_element_type=jnp.float32)


def matmul_nt(left_mat, right_mat):
    return lax.dot_general(left_mat, right_mat, NT_DIMS, preferred_element_type=jnp.float32)


def exact_dot(left_mat, right_mat):
    return jnp.dot(left_mat, right_mat, precision=EXACT, preferred_element_type=jnp.float32)


def precondition(a_inv, grad_mat, s_inv):
    return exact_dot(exact_dot(a_inv, grad_mat), s_inv)


def blend_factor(old_mats, first_new, second_new, inv_rows):
    return FACTOR_DECAY * old_mats + (1.0 - FACTOR_DECAY) * inv_rows * jnp.stack([first_new, second_new])


def local_pass(x_tokens, dy_tokens, w_col, w_row):
    z_one = matmul(x_tokens, w_col[0]).astype(jnp.bfloat16)
    h_one = activate(z_one)
    z_two = lax.psum(matmul(h_one, w_row[0]), 'model').astype(jnp.bfloat16)
    h_two = activate(z_two)
    z_three = matmul(h_two, w_col[1]).astype(jnp.bfloat16)
    h_three = activate(z_three)
    g_three = back_gate(matmul_nt(dy_tokens, w_row[1]).astype(jnp.bfloat16), z_three)
    dh_two = lax.psum(matmul_nt(g_three, w_col[1]), 'model').astype(jnp.bfloat16)
    g_two = back_gate(dh_two, z_two)
    g_one = back_gate(matmul_nt(g_two, w_row[0]).astype(jnp.bfloat16), z_one)
    return [x_tokens, h_one, h_two, h_three], [g_one, g_two, g_three, dy_tokens]


def finish_step(totals, inv_rows, a_old_col, s_old_col, a_old_row, s_old_row, a_inv_col, s_inv_col, a_inv_row, s_inv_row):
    weight_grads = [total_mat * inv_rows for total_mat in totals[8:]]
    u_col = jnp.stack([precondition(a_inv_col[0], weight_grads[0], s_inv_col[0]), precondition(a_inv_col[1], weight_grads[2], s_inv_col[1])])
    u_row = jnp.stack([precondition(a_inv_row[0], weight_grads[1], s_inv_row[0]), precondition(a_inv_row[1], weight_grads[3], s_inv_row[1])])
    a_new_col = blend_factor(a_old_col, totals[0], totals[2], inv_rows)
    s_new_col = blend_factor(s_old_col, totals[4], totals[6], inv_rows)
    a_new_row = blend_factor(a_old_row, totals[1], totals[3], inv_rows)
    s_new_row = blend_factor(s_old_row, totals[5], totals[7], inv_rows)
    return (u_col, u_row, a_new_col, s_new_col, a_new_row, s_new_row)


def solution(mesh):
    data_ways = mesh.shape['data']

    def shard_body(x_tokens, dy_tokens, w_col, w_row, a_old_col, s_old_col, a_old_row, s_old_row, a_inv_col, s_inv_col, a_inv_row, s_inv_row):
        layer_in, layer_grad = local_pass(x_tokens, dy_tokens, w_col, w_row)
        local_sums = [matmul_tn(layer_in[layer], layer_in[layer]) for layer in range(4)]
        local_sums += [matmul_tn(layer_grad[layer], layer_grad[layer]) for layer in range(4)]
        local_sums += [matmul_tn(layer_in[layer], layer_grad[layer]) for layer in range(4)]
        totals = lax.psum(local_sums, 'data')
        inv_rows = 1.0 / (x_tokens.shape[0] * data_ways)
        return finish_step(totals, inv_rows, a_old_col, s_old_col, a_old_row, s_old_row, a_inv_col, s_inv_col, a_inv_row, s_inv_row)

    batch_split = P('data', None)
    col_split = P(None, None, 'model')
    row_split = P(None, 'model', None)
    replicated = P()
    return jax.shard_map(
        shard_body,
        mesh=mesh,
        in_specs=(batch_split, batch_split, col_split, row_split, replicated, row_split, row_split, replicated, replicated, row_split, row_split, replicated),
        out_specs=(col_split, row_split, replicated, row_split, row_split, replicated),
        check_vma=False,
    )
```

profile of v0, /device:TPU:0, one launch (start us, length us, event | category | flops | bytes accessed | tf_op | source)
XLA Modules:
  0.0 5053.4 jit_solution(5203433838268368506)
XLA Ops:
  7.2 25.5 convolution_convert_fusion.2
  32.7 34.5 fusion.65
  67.2 1654.9 %all-reduce.10 = bf16[4096,3072]{1,0:T(8,128)(2,1)} all-reduce(f32[4096,3072]{1,0:T(8,128)} %fusion.65), channel_id=1, replica_groups=mesh['model'=4,'data'=2] {'model'}, use_global_device_ids=true, to_apply=%region_0.0 | all-reduce | flops 12582912 | bytes 75497472 | tf_op jit(solution)/shard_map/psum | solution.py:61
  1722.1 19.7 fusion.4
  1750.1 23.8 convolution_convert_fusion.1
  1773.9 90.3 %convolution_bitcast_fusion = f32[1,3072,3072]{2,1,0:T(8,128)} fusion(bf16[4096,3072]{1,0:T(8,128)(2,1)} %param.13), kind=kOutput, calls=%fused_computation.48 | convolution fusion | flops 77309411328 | bytes 62914560 | tf_op jit(solution)/shard_map/dot_general | solution.py:39
  1864.2 30.5 fusion.33
  1897.3 26.9 fusion.61
  1924.2 1645.8 %all-reduce.11 = bf16[4096,3072]{1,0:T(8,128)(2,1)} all-reduce(f32[4096,3072]{1,0:T(8,128)} %fusion.61), channel_id=1, replica_groups=mesh['model'=4,'data'=2] {'model'}, use_global_device_ids=true, to_apply=%region_1.0 | all-reduce | flops 12582912 | bytes 75497472 | tf_op jit(solution)/shard_map/psum | solution.py:66
  3570.0 38.9 fusion.9
  3609.0 90.3 %convolution_bitcast_fusion.1 = f32[1,3072,3072]{2,1,0:T(8,128)} fusion(bf16[4096,3072]{1,0:T(8,128)(2,1)} %fusion.9), kind=kOutput, calls=%fused_computation.49 | convolution fusion | flops 77309411328 | bytes 62914560 | tf_op jit(solution)/shard_map/dot_general | solution.py:39
  3709.5 32.5 fusion.40
  3752.4 16.3 convolution_bitcast_fusion.7
  3768.7 11.1 convolution_bitcast_fusion.8
  3779.8 26.8 convolution_bitcast_fusion.6
  3806.6 25.8 fusion.95
  3832.4 33.4 fusion.92
  3865.8 26.6 fusion.98
  3892.4 90.3 %convolution_bitcast_fusion.2 = f32[1,3072,3072]{2,1,0:T(8,128)} fusion(bf16[4096,3072]{1,0:T(8,128)(2,1)} %copy-done), kind=kOutput, calls=%fused_computation.50 | convolution fusion | flops 77309411328 | bytes 62914560 | tf_op jit(solution)/shard_map/dot_general | solution.py:39
  3982.7 89.9 %convolution_bitcast_fusion.3 = f32[1,3072,3072]{2,1,0:T(8,128)} fusion(bf16[4096,3072]{1,0:T(8,128)(2,1)} %param.12), kind=kOutput, calls=%fused_computation.51 | convolution fusion | flops 77309411328 | bytes 62914560 | tf_op jit(solution)/shard_map/dot_general | solution.py:39
  4072.7 72.1 %fusion.1 = f32[2,3072,3072]{2,1,0:T(8,128)} fusion(f32[1,3072,3072]{2,1,0:T(8,128)} %get-tuple-element.16, f32[1,3072,3072]{2,1,0:T(8,128)} %get-tuple-element.17, f32[2,3072,3072]{2,1,0:T(8,128)} %param.19), kind=kLoop, calls=%fused_computation.10 | loop fusion | flops 75497472 | bytes 226492416 | tf_op jit(solution)/shard_map/add | solution.py:55
  4144.8 238.2 %all-reduce.7.cloned.1.call-done = (f32[3072,768]{0,1:T(8,128)}, f32[3072,768]{0,1:T(8,128)}, f32[768,3072]{1,0:T(8,128)}, f32[768,3072]{1,0:T(8,128)}, f32[1,30...) async-done(((f32[3072,768]{0,1:T(8,128)}, ...) | async-done | bytes 122683408 | tf_op jit(solution)/shard_map/psum | solution.py:91
  4383.0 49.3 fusion.49
  4432.2 62.8 %fusion.47 = f32[3072,768]{1,0:T(8,128)} fusion(f32[768,3072]{1,0:T(8,128)S(1)} %copy-done.3, f32[2,768,768]{2,1,0:T(8,128)S(1)} %copy-done.4), kind=kOutput, calls=%fused_computation.76 | convolution fusion | flops 21745631232 | bytes 21233664 | tf_op jit(solution)/shard_map/dot_general | solution.py:47
  4495.1 100.1 %fusion.53 = f32[1,768,3072]{2,1,0:T(8,128)} fusion(f32[3072,768]{1,0:T(8,128)} %fusion.49, f32[2,3072,3072]{2,1,0:T(8,128)} %param.23), kind=kOutput, calls=%fused_computation.88 | convolution fusion | flops 86973087744 | bytes 56623104 | tf_op jit(solution)/shard_map/dot_general | solution.py:47
  4595.2 100.3 %fusion.56 = f32[1,768,3072]{2,1,0:T(8,128)} fusion(f32[3072,768]{1,0:T(8,128)} %fusion.47, f32[2,3072,3072]{2,1,0:T(8,128)} %param.23), kind=kOutput, calls=%fused_computation.89 | convolution fusion | flops 86973087744 | bytes 56623104 | tf_op jit(solution)/shard_map/dot_general | solution.py:47
  4695.5 96.8 %fusion.17 = f32[768,3072]{1,0:T(8,128)} fusion(f32[2,3072,3072]{2,1,0:T(8,128)} %param.20, f32[3072,768]{0,1:T(8,128)} %get-tuple-element.6), kind=kOutput, calls=%fused_computation.26 | convolution fusion | flops 86975447040 | bytes 56623104 | tf_op jit(solution)/shard_map/dot_general | solution.py:47
  4792.3 96.7 %fusion.19 = f32[768,3072]{1,0:T(8,128)} fusion(f32[2,3072,3072]{2,1,0:T(8,128)} %param.20, f32[3072,768]{0,1:T(8,128)} %get-tuple-element.7), kind=kOutput, calls=%fused_computation.28 | convolution fusion | flops 86975447040 | bytes 56623104 | tf_op jit(solution)/shard_map/dot_general | solution.py:47
  4889.1 29.5 convolution_bitcast_fusion.4
  4918.6 27.4 convolution_bitcast_fusion.5
  4953.0 10.9 pad_maximum_fusion
  4963.9 72.2 %fusion = f32[2,3072,3072]{2,1,0:T(8,128)} fusion(f32[1,3072,3072]{2,1,0:T(8,128)} %get-tuple-element.10, f32[1,3072,3072]{2,1,0:T(8,128)} %get-tuple-element.11, f32[2,3072,3072]{2,1,0:T(8,128)} %param.16), kind=kLoop, calls=%fused_computation.8 | loop fusion | flops 75497472 | bytes 226492416 | tf_op jit(solution)/shard_map/add | solution.py:55
  (58 shorter events, 48.8 us)
Async XLA Ops:
  7.2 4065.5 %all-reduce.9.cloned.1.call-start = ((), (), s32[]{:S(2)}) async-start(), calls=%async_computation.1 | async-start | bytes 150994944 | tf_op jit(solution)/shard_map/psum | solution.py:91
  1741.8 8.3 copy-start
  1894.7 2.6 copy-start.5
  3699.3 683.7 %all-reduce.7.cloned.1.call-start = ((), (), s32[]{:S(2)}) async-start(), calls=%async_computation | async-start | bytes 245366784 | tf_op jit(solution)/shard_map/psum | solution.py:91
  3699.3 10.2 copy-start.2
  3742.0 26.6 slice-start.14
  3752.4 16.3 slice-start.15
  3768.7 37.9 slice-start
  3768.7 37.9 slice-start.1
  3768.7 37.9 slice-start.2
  3779.8 26.8 slice-start.3
  3779.8 26.8 slice-start.4
  3779.8 26.8 slice-start.5
  4383.0 49.3 copy-start.3
  4383.0 49.3 copy-start.4
  4695.5 193.6 %slice-start.12 = ((s8[4718592]{0:T(1024)(128)(4,1)}), s8[4194304]{0:T(1024)(128)(4,1)S(1)}, s32[]{:S(2)}) async-start(s8[4718592]{0:T(1024)(128)(4,1)} %bitcast.117), calls=%async_computation.14 | async-start | bytes 8388608
  4792.3 96.7 %slice-start.13 = ((s8[4718592]{0:T(1024)(128)(4,1)}), s8[524288]{0:T(1024)(128)(4,1)S(1)}, s32[]{:S(2)}) async-start(s8[4718592]{0:T(1024)(128)(4,1)} %bitcast.117), calls=%async_computation.15 | async-start | bytes 1048576
  4889.1 57.0 %slice-start.6 = ((s8[9437184]{0:T(1024)(128)(4,1)}), s8[4194304]{0:T(1024)(128)(4,1)S(1)}, s32[]{:S(2)}) async-start(s8[9437184]{0:T(1024)(128)(4,1)} %bitcast.113), calls=%async_computation.8 | async-start | bytes 8388608
  4889.1 57.0 %slice-start.7 = ((s8[9437184]{0:T(1024)(128)(4,1)}), s8[4194304]{0:T(1024)(128)(4,1)S(1)}, s32[]{:S(2)}) async-start(s8[9437184]{0:T(1024)(128)(4,1)} %bitcast.113), calls=%async_computation.9 | async-start | bytes 8388608
  4889.1 57.0 %slice-start.9 = ((s8[9437184]{0:T(1024)(128)(4,1)}), s8[4194304]{0:T(1024)(128)(4,1)S(1)}, s32[]{:S(2)}) async-start(s8[9437184]{0:T(1024)(128)(4,1)} %bitcast.115), calls=%async_computation.11 | async-start | bytes 8388608
  4889.1 57.0 %slice-start.10 = ((s8[9437184]{0:T(1024)(128)(4,1)}), s8[4194304]{0:T(1024)(128)(4,1)S(1)}, s32[]{:S(2)}) async-start(s8[9437184]{0:T(1024)(128)(4,1)} %bitcast.115), calls=%async_computation.12 | async-start | bytes 8388608
  4918.6 27.5 slice-start.8
  4918.6 27.5 slice-start.11
  4963.9 72.2 %copy-start.1 = (f32[1,768,768]{2,1,0:T(8,128)S(1)}, f32[1,768,768]{2,1,0:T(8,128)}, u32[]{:S(2)}) copy-start(f32[1,768,768]{2,1,0:T(8,128)} %get-tuple-element.12) | copy-start | bytes 7077892
Sparse Core Ops, SparseCore 0:
  3699.4 178.1 all-reduce.8
  4072.8 310.1 all-reduce.6
where the time goes:
time: 5060 us; the launch traced here: 5050 us
  blocking collectives  3300 us (65%)
  matrix products  1260 us (25%)
  waiting for transfers between devices  238 us (5%)
  other arithmetic  231 us (5%)
    psum x1, blocking collectives, local_pass(): z_two = lax.psum(matmul(h_one, w_row[0]), 'model').astype(jnp.bfloat16)  1650 us
    psum x1, blocking collectives, local_pass(): lax.psum(matmul_nt(g_three, w_col[1]), 'model').astype(jnp.bfloat16)  1650 us
    dot_general x8, matrix products, exact_dot(): jnp.dot(left_mat, right_mat, precision=EXACT, preferred_element_type=jnp....  563 us
    dot_general x12, matrix products, matmul_tn(): lax.dot_general(left_mat, right_mat, TN_DIMS, preferred_element_type=jnp....  521 us
    psum x2, waiting for transfers between devices, shard_body(): totals = lax.psum(local_sums, 'data')  238 us
    add x3, other arithmetic, blend_factor(): FACTOR_DECAY * old_mats  154 us
  transfers between devices with their start and end apart: 2, of which 1 were waited for; matrix products, arithmetic and copies ran while one was open for 9% of the time, Pallas kernels for 0%

commit v1 on v0

v1 whole, which is shorter than its diff:
```python
import math
import jax
import jax.numpy as jnp
from jax import lax
from jax.sharding import PartitionSpec as P

FACTOR_DECAY = 0.8
GELU_SCALE = math.sqrt(2.0 / math.pi)
GELU_CUBIC = 0.044715
EXACT = lax.Precision.HIGHEST
TN_DIMS = (((0,), (0,)), ((), ()))
NT_DIMS = (((1,), (1,)), ((), ()))


def gelu_value(pre_act):
    tanh_arg = GELU_SCALE * (pre_act + GELU_CUBIC * pre_act * pre_act * pre_act)
    return 0.5 * pre_act * (1.0 + jnp.tanh(tanh_arg))


def gelu_slope(pre_act):
    tanh_arg = GELU_SCALE * (pre_act + GELU_CUBIC * pre_act * pre_act * pre_act)
    tanh_val = jnp.tanh(tanh_arg)
    return 0.5 * (1.0 + tanh_val) + 0.5 * pre_act * (1.0 - tanh_val * tanh_val) * GELU_SCALE * (1.0 + 3.0 * GELU_CUBIC * pre_act * pre_act)


def activate(pre_act):
    return gelu_value(pre_act.astype(jnp.float32)).astype(jnp.bfloat16)


def back_gate(grad_act, pre_act):
    return (grad_act.astype(jnp.float32) * gelu_slope(pre_act.astype(jnp.float32))).astype(jnp.bfloat16)


def matmul(left_mat, right_mat):
    return jnp.dot(left_mat, right_mat, preferred_element_type=jnp.float32)


def matmul_tn(left_mat, right_mat):
    return lax.dot_general(left_mat, right_mat, TN_DIMS, preferred_element_type=jnp.float32)


def matmul_nt(left_mat, right_mat):
    return lax.dot_general(left_mat, right_mat, NT_DIMS, preferred_element_type=jnp.float32)


def exact_dot(left_mat, right_mat):
    return jnp.dot(left_mat, right_mat, precision=EXACT, preferred_element_type=jnp.float32)


def blend_factor(old_mats, first_new, second_new, inv_rows):
    return FACTOR_DECAY * old_mats + (1.0 - FACTOR_DECAY) * inv_rows * jnp.stack([first_new, second_new])


def solution(mesh):
    data_ways = mesh.shape['data']
    model_ways = mesh.shape['model']

    def to_rows(col_part):
        return lax.all_to_all(col_part, 'model', split_axis=0, concat_axis=1, tiled=True)

    def gather_weight(part):
        half = part.shape[0] // data_ways
        mine = lax.dynamic_slice_in_dim(part, lax.axis_index('data') * half, half, 0)
        return lax.all_gather(mine, ('model', 'data'), axis=0, tiled=True)

    def precondition_col(a_inv, grad_half, s_inv):
        half_rows = grad_half.shape[0]
        right_done = lax.all_gather(exact_dot(grad_half, s_inv), 'data', axis=0, tiled=True)
        a_rows = lax.dynamic_slice_in_dim(a_inv, lax.axis_index('data') * half_rows, half_rows, 0)
        return lax.all_gather(exact_dot(a_rows, right_done), 'data', axis=0, tiled=True)

    def precondition_row(a_inv, grad_half, s_inv):
        half_cols = grad_half.shape[1]
        left_done = lax.all_gather(exact_dot(a_inv, grad_half), 'data', axis=1, tiled=True)
        s_cols = lax.dynamic_slice_in_dim(s_inv, lax.axis_index('data') * half_cols, half_cols, 1)
        return lax.all_gather(exact_dot(left_done, s_cols), 'data', axis=1, tiled=True)

    def shard_body(x_tokens, dy_tokens, w_col, w_row, a_old_col, s_old_col, a_old_row, s_old_row, a_inv_col, s_inv_col, a_inv_row, s_inv_row):
        inv_rows = 1.0 / (x_tokens.shape[0] * data_ways)
        w_two = gather_weight(w_row[0])
        w_three_t = gather_weight(w_col[1].T)
        z_one = matmul(x_tokens, w_col[0]).astype(jnp.bfloat16)
        h_one = activate(z_one)
        dh_three = matmul_nt(dy_tokens, w_row[1]).astype(jnp.bfloat16)
        h_one_t = to_rows(h_one)
        dh_three_t = to_rows(dh_three)
        z_two_t = matmul(h_one_t, w_two).astype(jnp.bfloat16)
        h_two_t = activate(z_two_t)
        h_two = lax.all_gather(h_two_t, 'model', axis=0, tiled=True)
        a_one = matmul_tn(x_tokens, x_tokens)
        a_two = matmul_tn(h_one, h_one)
        z_three_t = matmul_nt(h_two_t, w_three_t).astype(jnp.bfloat16)
        g_three_t = back_gate(dh_three_t, z_three_t)
        dh_two_t = matmul(g_three_t, w_three_t).astype(jnp.bfloat16)
        g_two_t = back_gate(dh_two_t, z_two_t)
        g_two = lax.all_gather(g_two_t, 'model', axis=0, tiled=True)


        h_two, a_one, a_two, g_two_t = lax.optimization_barrier((h_two, a_one, a_two, g_two_t))
        z_three = matmul(h_two, w_col[1]).astype(jnp.bfloat16)
        h_three = activate(z_three)
        g_three = back_gate(dh_three, z_three)
        grad_four = matmul_tn(h_three, dy_tokens)
        grad_three = matmul_tn(h_two, g_three)
        a_three = matmul_tn(h_two, h_two)
        a_four = matmul_tn(h_three, h_three)
        s_three = matmul_tn(g_three, g_three)
        s_four = matmul_tn(dy_tokens, dy_tokens)
        g_two, grad_three, grad_four, a_one, a_two, a_three, a_four, s_three, s_four = lax.optimization_barrier(
            (g_two, grad_three, grad_four, a_one, a_two, a_three, a_four, s_three, s_four))
        grad_four = lax.psum_scatter(grad_four, 'data', scatter_dimension=1, tiled=True) * inv_rows
        grad_three = lax.psum_scatter(grad_three, 'data', scatter_dimension=0, tiled=True) * inv_rows

        g_one = back_gate(matmul_nt(g_two, w_row[0]).astype(jnp.bfloat16), z_one)
        grad_one = lax.psum_scatter(matmul_tn(x_tokens, g_one), 'data', scatter_dimension=0, tiled=True) * inv_rows
        grad_two = lax.psum_scatter(matmul_tn(h_one, g_two), 'data', scatter_dimension=1, tiled=True) * inv_rows
        s_two = matmul_tn(g_two, g_two)
        s_one = matmul_tn(g_one, g_one)
        a_one, a_two, a_three, a_four, s_three, s_four = lax.psum([a_one, a_two, a_three, a_four, s_three, s_four], 'data')
        s_one, s_two, a_one, a_two, a_three, a_four, s_three, s_four = lax.optimization_barrier(
            (s_one, s_two, a_one, a_two, a_three, a_four, s_three, s_four))
        s_one, s_two = lax.psum([s_one, s_two], 'data')

        u_col = jnp.stack([precondition_col(a_inv_col[0], grad_one, s_inv_col[0]), precondition_col(a_inv_col[1], grad_three, s_inv_col[1])])
        u_row = jnp.stack([precondition_row(a_inv_row[0], grad_two, s_inv_row[0]), precondition_row(a_inv_row[1], grad_four, s_inv_row[1])])
        a_new_col = blend_factor(a_old_col, a_one, a_three, inv_rows)
        s_new_col = blend_factor(s_old_col, s_one, s_three, inv_rows)
        a_new_row = blend_factor(a_old_row, a_two, a_four, inv_rows)
        s_new_row = blend_factor(s_old_row, s_two, s_four, inv_rows)
        return (u_col, u_row, a_new_col, s_new_col, a_new_row, s_new_row)

    batch_split = P('data', None)
    col_split = P(None, None, 'model')
    row_split = P(None, 'model', None)
    replicated = P()
    return jax.shard_map(
        shard_body,
        mesh=mesh,
        in_specs=(batch_split, batch_split, col_split, row_split, replicated, row_split, row_split, replicated, replicated, row_split, row_split, replicated),
        out_specs=(col_split, row_split, replicated, row_split, row_split, replicated),
        check_vma=False,
    )
```

time: 5060 us -> 1590 us (0.31)
  blocking collectives: 3300 us -> 119 us
  matrix products: 1260 us -> 1030 us
  waiting for transfers between devices: 238 us -> 76.2 us
  local copies, waits for them, and re-layouts: 11 us -> 143 us
    psum x2 -> x0, blocking collectives: 3300 us -> none  [the longest x1 1650 us: local_pass(): z_two = lax.psum(matmul(h_one, w_row[0]), 'model').astype(jnp.bfloat16)]
    dot_general x8, matrix products: 563 us -> 290 us  [exact_dot(): jnp.dot(left_mat, right_mat, precision=EXACT, preferred_element_type=jnp....]
    psum x2, waiting for transfers between devices: 238 us -> 15 us  [the longest x1 15 us: shard_body(): s_one, s_two = lax.psum([s_one, s_two], 'data')]
    all_to_all x0 -> x1, blocking collectives: none -> 119 us  [to_rows(): lax.all_to_all(col_part, 'model', split_axis=0, concat_axis=1, tiled=True)]
    slice x0 -> x4, local copies, waits for them, and re-layouts: none -> 112 us  [the longest x1 52.5 us: shard_body(): a_inv_col[0]]
    convert_element_type x2 -> x0, other arithmetic: 58.6 us -> none  [the longest x1 38.9 us: back_gate(): (grad_act.astype(jnp.float32) * gelu_slope(pre_act.astype(jnp.float32)))....]
    dot_general x3 -> x4, matrix products: 83.7 us -> 138 us  [matmul(): return jnp.dot(left_mat, right_mat, preferred_element_type=jnp.float32)]
    add x3 -> x4, other arithmetic: 154 us -> 153 us  [blend_factor(): FACTOR_DECAY * old_mats]
  transfers between devices with their start and end apart: 2 -> 19, of which waited for: 1 -> 6; matrix products, arithmetic and copies ran while one was open for 9% -> 77% of each run, Pallas kernels for 0% -> 0%
where the time goes in v1:
time: 1590 us; the launch traced here: 1580 us
  matrix products  1030 us (65%)
  other arithmetic  191 us (12%)
  local copies, waits for them, and re-layouts  143 us (9%)
  blocking collectives  119 us (7%)
  waiting for transfers between devices  76.2 us (5%)
    dot_general x12, matrix products, matmul_tn(): lax.dot_general(left_mat, right_mat, TN_DIMS, preferred_element_type=jnp....  509 us
    dot_general x8, matrix products, exact_dot(): jnp.dot(left_mat, right_mat, precision=EXACT, preferred_element_type=jnp....  290 us
    add x4, other arithmetic, blend_factor(): FACTOR_DECAY * old_mats  153 us
    dot_general x4, matrix products, matmul(): return jnp.dot(left_mat, right_mat, preferred_element_type=jnp.float32)  138 us
    all_to_all x1, blocking collectives, to_rows(): lax.all_to_all(col_part, 'model', split_axis=0, concat_axis=1, tiled=True)  119 us
    dot_general x3, matrix products, matmul_nt(): lax.dot_general(left_mat, right_mat, NT_DIMS, preferred_element_type=jnp....  92.2 us
    slice x1, local copies, waits for them, and re-layouts, shard_body(): a_inv_col[0]  52.5 us
    slice x1, local copies, waits for them, and re-layouts, shard_body(): s_inv_row[0]  52.2 us
  transfers between devices with their start and end apart: 19, of which 6 were waited for; matrix products, arithmetic and copies ran while one was open for 77% of the time, Pallas kernels for 0%

profile of v1, /device:TPU:0, one launch (start us, length us, event | category | flops | bytes accessed | tf_op | source)
XLA Modules:
  0.0 1579.1 jit_solution(9831578330622775312)
XLA Ops:
  19.7 29.7 %fusion.34 = (bf16[4096,768]{1,0:T(8,128)(2,1)}, bf16[4096,768]{1,0:T(8,128)(2,1)}) fusion(bf16[4096,3072]{1,0:T(8,128)(2,1)} %param.12, bf16[2,3072,768]{2,1,0:T(8,128)(2,1)} %param.14), kind=kOutput, calls=%fused_computation.66 | convolution fusion | flops 19361955840 | bytes 42467328 | tf_op jit(solution)/shard_map/dot_general | solution.py:35
  58.1 118.6 %all_to_all.32 = bf16[4,1024,768]{1,2,0:T(8,128)(2,1)} all-to-all(bf16[4,1024,768]{1,2,0:T(8,128)(2,1)} %copy.20), channel_id=1, replica_groups=mesh['model'=4,'data'=2] {'model'}, dimensions={0} | all-to-all | bytes 12582912 | tf_op jit(solution)/shard_map/all_to_all | solution.py:59
  178.1 29.2 %fusion.28 = (bf16[1024,3072]{1,0:T(8,128)(2,1)}, bf16[1024,3072]{1,0:T(8,128)(2,1)}) fusion(bf16[1024,3072]{0,1:T(8,128)(2,1)} %bitcast.124, bf16[1,3072,3072]{2,1,0:T(8,128)(2,1)} %all-gather.36.cloned.1.call-done), kind=kOutput, calls=%fused_computation.60 | convolution fusion | flops 19361955840 | bytes 37748736 | tf_op jit(solution)/shard_map/dot_general | solution.py:35
  207.3 25.6 %convolution_convert_fusion.3 = bf16[4096,768]{1,0:T(8,128)(2,1)} fusion(bf16[4096,3072]{1,0:T(8,128)(2,1)} %param.13, bf16[2,768,3072]{2,1,0:T(8,128)(2,1)} %param.15), kind=kOutput, calls=%fused_computation.94 | convolution fusion | flops 19330498560 | bytes 36175872 | tf_op jit(solution)/shard_map/dot_general | solution.py:43
  238.2 90.5 %fusion.122 = f32[3072,3072]{1,0:T(8,128)} fusion(bf16[4096,3072]{1,0:T(8,128)(2,1)} %param.12), kind=kOutput, calls=%fused_computation.152 | convolution fusion | flops 77309411328 | bytes 62914560 | tf_op jit(solution)/shard_map/dot_general | solution.py:39
  358.8 36.2 %fusion.118 = bf16[1024,3072]{1,0:T(8,128)(2,1)} fusion(bf16[3072,3072]{0,1:T(8,128)(2,1)} %all-gather.14.cloned.1.call-done, bf16[1024,3072]{1,0:T(8,128)(2,1)} %get-tuple-element.61), kind=kOutput, calls=%fused_computation.149 | convolution fusion | flops 19358810112 | bytes 31457280 | tf_op jit(solution)/shard_map/dot_general | solution.py:43
  395.0 45.0 %fusion.33 = bf16[1024,3072]{1,0:T(8,128)(2,1)} fusion(bf16[1024,3072]{1,0:T(8,128)(2,1)} %get-tuple-element.61, bf16[3072,3072]{0,1:T(8,128)(2,1)} %all-gather.14.cloned.1.call-done, f32[1024,3072]{1,0:T(8,128)} %bitcast.117, bf16[1024,3072]{1,0:T(8,128)(2,1)} %fusion.118), kind=kOutput, calls=%fused_computation.65 | convolution fusion | flops 19459473408 | bytes 50331648 | tf_op jit(solution)/shard_map/dot_general | solution.py:35
  440.0 90.3 %fusion.127 = f32[3072,3072]{1,0:T(8,128)} fusion(bf16[4096,3072]{1,0:T(8,128)(2,1)} %param.13), kind=kOutput, calls=%fused_computation.157 | convolution fusion | flops 77309411328 | bytes 62914560 | tf_op jit(solution)/shard_map/dot_general | solution.py:39
  540.4 25.1 %all-gather.18.cloned.1.call-done = bf16[4096,3072]{1,0:T(8,128)(2,1)} async-done(((bf16[1024,3072]{1,0:T(8,128)(2,1)}), bf16[4096,3072]{1,0:T(8,128)(2,1)}) %all-gather.18.cloned.1.call-update) | async-done | bytes 25165840 | tf_op jit(solution)/shard_map/all_gather | solution.py:89
  565.6 34.2 %fusion.26 = (bf16[4096,768]{1,0:T(8,128)(2,1)S(1)}, bf16[4096,768]{1,0:T(8,128)(2,1)}) fusion(bf16[4096,768]{1,0:T(8,128)(2,1)} %convolution_convert_fusion.3, bf16[4096,3072]{1,0:T(8,128)(2,1)} %all-gather.18.cloned.1.call-done, bf16[2,3072,768]{2,1,0:T(8,128)(2,1)} %param.14), kind=kOutput, calls=%fused_computation.58 | convolution fusion | flops 19396558848 | bytes 48758784 | tf_op jit(solution)/shard_map/dot_general | solution.py:35
  609.1 16.7 %fusion.112 = f32[768,768]{1,0:T(8,128)} fusion(bf16[4096,768]{1,0:T(8,128)(2,1)} %get-tuple-element.63), kind=kOutput, calls=%fused_computation.145 | convolution fusion | flops 4863295488 | bytes 8650752 | tf_op jit(solution)/shard_map/dot_general | solution.py:39
  625.9 25.4 %fusion.114 = f32[768,3072]{1,0:T(8,128)} fusion(bf16[4096,3072]{1,0:T(8,128)(2,1)S(1)} %bitcast.132, bf16[4096,768]{1,0:T(8,128)(2,1)} %get-tuple-element.63), kind=kOutput, calls=%fused_computation.146 | convolution fusion | flops 19358810112 | bytes 40894464 | tf_op jit(solution)/shard_map/dot_general | solution.py:39
  651.3 26.8 %fusion.124 = f32[3072,768]{1,0:T(8,128)} fusion(bf16[4096,3072]{1,0:T(8,128)(2,1)} %all-gather.18.cloned.1.call-done, bf16[4096,768]{1,0:T(8,128)(2,1)} %copy-done.4), kind=kOutput, calls=%fused_computation.154 | convolution fusion | flops 19327352832 | bytes 40894464 | tf_op jit(solution)/shard_map/dot_general | solution.py:39
  678.0 90.2 %fusion.125 = f32[3072,3072]{1,0:T(8,128)} fusion(bf16[4096,3072]{1,0:T(8,128)(2,1)} %all-gather.18.cloned.1.call-done), kind=kOutput, calls=%fused_computation.155 | convolution fusion | flops 77309411328 | bytes 62914560 | tf_op jit(solution)/shard_map/dot_general | solution.py:39
  768.3 21.1 %all-gather.16.cloned.1.call-done = bf16[4096,3072]{1,0:T(8,128)(2,1)} async-done(((bf16[1024,3072]{1,0:T(8,128)(2,1)}), bf16[4096,3072]{1,0:T(8,128)(2,1)}) %all-gather.16.cloned.1.call-update) | async-done | bytes 25165840 | tf_op jit(solution)/shard_map/all_gather | solution.py:96
  789.4 30.5 %fusion.39 = bf16[4096,768]{1,0:T(8,128)(2,1)S(1)} fusion(bf16[4096,768]{1,0:T(8,128)(2,1)} %get-tuple-element.59, bf16[4096,3072]{1,0:T(8,128)(2,1)} %all-gather.16.cloned.1.call-done, bf16[2,768,3072]{2,1,0:T(8,128)(2,1)} %param.15), kind=kOutput, calls=%fused_computation.71 | convolution fusion | flops 19396558848 | bytes 42467328 | tf_op jit(solution)/shard_map/dot_general | solution.py:43
  822.5 25.4 %convolution_bitcast_fusion = f32[3072,768]{1,0:T(8,128)} fusion(bf16[4096,768]{1,0:T(8,128)(2,1)S(1)} %fusion.39, bf16[4096,3072]{1,0:T(8,128)(2,1)} %param.12), kind=kOutput, calls=%fused_computation.97 | convolution fusion | flops 19327352832 | bytes 40894464 | tf_op jit(solution)/shard_map/dot_general | solution.py:39
  848.6 26.8 %fusion.128 = f32[768,3072]{1,0:T(8,128)} fusion(bf16[4096,768]{1,0:T(8,128)(2,1)} %get-tuple-element.58, bf16[4096,3072]{1,0:T(8,128)(2,1)} %all-gather.16.cloned.1.call-done), kind=kOutput, calls=%fused_computation.158 | convolution fusion | flops 19327352832 | bytes 40894464 | tf_op jit(solution)/shard_map/dot_general | solution.py:39
  876.2 15.5 fusion.77
  891.8 15.5 fusion.75
  907.4 26.6 %fusion.81 = f32[768,1536]{0,1:T(8,128)} fusion(f32[768,1536]{1,0:T(8,128)} %reduce-scatter.9.cloned.1.call-done, f32[2,768,768]{2,1,0:T(8,128)} %param.22), kind=kOutput, calls=%fused_computation.116 | convolution fusion | flops 10872815616 | bytes 11796480 | tf_op jit(solution)/shard_map/dot_general | solution.py:47
  934.0 26.3 %fusion.84 = f32[768,1536]{0,1:T(8,128)} fusion(f32[768,1536]{1,0:T(8,128)} %reduce-scatter.11.cloned.1.call-done, f32[2,768,768]{2,1,0:T(8,128)} %param.22), kind=kOutput, calls=%fused_computation.117 | convolution fusion | flops 10872815616 | bytes 11796480 | tf_op jit(solution)/shard_map/dot_general | solution.py:47
  961.2 52.5 %fusion.121 = (f32[1,3072,3072]{2,1,0:T(8,128)}, f32[1,3072,3072]{2,1,0:T(8,128)}) fusion(f32[2,3072,3072]{2,1,0:T(8,128)} %param.20), kind=kLoop, calls=%fused_computation.151 | loop fusion | bytes 150994944 | tf_op jit(solution)/shard_map/slice | solution.py:124
  1013.6 52.0 %fusion.10 = f32[1536,768]{1,0:T(8,128)} fusion(f32[3072,768]{1,0:T(8,128)} %all-gather.20.cloned.1.call-done, f32[1,3072,3072]{2,1,0:T(8,128)} %get-tuple-element.56, s32[]{:T(128)S(6)} %select_n.4), kind=kOutput, calls=%fused_computation.42 | convolution fusion | flops 43486543872 | bytes 33030148 | tf_op jit(solution)/shard_map/dot_general | solution.py:47
  1065.7 52.0 %fusion.6 = f32[1536,768]{1,0:T(8,128)} fusion(f32[3072,768]{1,0:T(8,128)} %all-gather.24.cloned.1.call-done, f32[1,3072,3072]{2,1,0:T(8,128)} %get-tuple-element.57, s32[]{:T(128)S(6)} %select_n.4), kind=kOutput, calls=%fused_computation.38 | convolution fusion | flops 43486543872 | bytes 33030148 | tf_op jit(solution)/shard_map/dot_general | solution.py:47
  1117.8 52.2 %fusion.120 = (f32[1,3072,3072]{2,1,0:T(8,128)}, f32[1,3072,3072]{2,1,0:T(8,128)}) fusion(f32[2,3072,3072]{2,1,0:T(8,128)} %param.23), kind=kLoop, calls=%fused_computation.150 | loop fusion | bytes 150994944 | tf_op jit(solution)/shard_map/slice | solution.py:125
  1170.1 51.2 %fusion.4 = f32[768,1536]{1,0:T(8,128)} fusion(f32[768,3072]{0,1:T(8,128)} %all-gather.28.cloned.1.call-done, f32[1,3072,3072]{2,1,0:T(8,128)} %get-tuple-element.54, s32[]{:T(128)S(6)} %select_n.4), kind=kOutput, calls=%fused_computation.36 | convolution fusion | flops 43486543872 | bytes 33030148 | tf_op jit(solution)/shard_map/dot_general | solution.py:47
  1221.3 51.0 %fusion.2 = f32[768,1536]{1,0:T(8,128)} fusion(f32[768,3072]{0,1:T(8,128)} %all-gather.32.cloned.1.call-done, f32[1,3072,3072]{2,1,0:T(8,128)} %get-tuple-element.55, s32[]{:T(128)S(6)} %select_n.4), kind=kOutput, calls=%fused_computation.34 | convolution fusion | flops 43486543872 | bytes 33030148 | tf_op jit(solution)/shard_map/dot_general | solution.py:47
  1272.4 90.3 %fusion.130 = f32[3072,3072]{1,0:T(8,128)} fusion(bf16[4096,3072]{1,0:T(8,128)(2,1)} %all-gather.16.cloned.1.call-done), kind=kOutput, calls=%fused_computation.160 | convolution fusion | flops 77309411328 | bytes 62914560 | tf_op jit(solution)/shard_map/dot_general | solution.py:39
  1406.5 72.2 %fusion = f32[2,3072,3072]{2,1,0:T(8,128)} fusion(f32[1,3072,3072]{2,1,0:T(8,128)} %bitcast.115, f32[1,3072,3072]{2,1,0:T(8,128)} %bitcast.114, f32[2,3072,3072]{2,1,0:T(8,128)} %param.16), kind=kLoop, calls=%fused_computation.1 | loop fusion | flops 75497472 | bytes 226492416 | tf_op jit(solution)/shard_map/add | solution.py:51
  1478.8 15.0 all-reduce.5.cloned.1.call-done
  1499.8 72.1 %fusion.1 = f32[2,3072,3072]{2,1,0:T(8,128)} fusion(f32[1,3072,3072]{2,1,0:T(8,128)} %bitcast.113, f32[1,3072,3072]{2,1,0:T(8,128)} %get-tuple-element.47, f32[2,3072,3072]{2,1,0:T(8,128)} %param.19), kind=kLoop, calls=%fused_computation.3 | loop fusion | flops 75497472 | bytes 226492416 | tf_op jit(solution)/shard_map/add | solution.py:51
  (95 shorter events, 132.7 us)
Async XLA Ops:
  7.2 170.9 %all-gather.36.cloned.1.call-start = ((), (), s32[]{:S(2)}) async-start(), calls=%async_computation.21 | async-start | bytes 21233664 | tf_op jit(solution)/shard_map/all_gather | solution.py:64
  15.3 343.5 %all-gather.14.cloned.1.call-start = ((), (), s32[]{:S(2)}) async-start(), calls=%async_computation.6 | async-start | bytes 21233664 | tf_op jit(solution)/shard_map/all_gather | solution.py:64
  19.7 545.9 %all-gather.18.cloned.1.call-start = ((), (), s32[]{:S(2)}) async-start(), calls=%async_computation.8 | async-start | bytes 31457280 | tf_op jit(solution)/shard_map/all_gather | solution.py:89
  232.9 106.0 %all-to-all-start = ((bf16[4,1024,768]{2,1,0:T(8,128)(2,1)}), bf16[4,1024,768]{2,1,0:T(8,128)(2,1)}, u32[]{:S(2)}, u32[]{:S(2)}) async-start(bf16[4,1024,768]{2,1,0:T(8,128)(2,1)} %bitcast.123), calls=%async_computation | async-start | bytes 12582912 | tf_op jit(solution)/shard_map/all_to_all | solution.py:59
  238.1 551.2 %all-gather.16.cloned.1.call-start = ((), (), s32[]{:S(2)}) async-start(), calls=%async_computation.7 | async-start | bytes 31457280 | tf_op jit(solution)/shard_map/all_gather | solution.py:96
  440.0 436.2 %reduce-scatter.5.cloned.1.call-start = ((), (), s32[]{:S(2)}) async-start(), calls=%async_computation.9 | async-start | bytes 14155776 | tf_op jit(solution)/shard_map/reduce_scatter | solution.py:115
  599.8 2.7 copy-start.4
  602.5 23.4 %slice-start.2 = ((s8[25165824]{0:T(1024)(128)(4,1)}), s8[4194304]{0:T(1024)(128)(4,1)S(1)}, s32[]{:S(2)}) async-start(s8[25165824]{0:T(1024)(128)(4,1)} %bitcast.131), calls=%async_computation.26 | async-start | bytes 8388608
  602.5 23.4 %slice-start.3 = ((s8[25165824]{0:T(1024)(128)(4,1)}), s8[4194304]{0:T(1024)(128)(4,1)S(1)}, s32[]{:S(2)}) async-start(s8[25165824]{0:T(1024)(128)(4,1)} %bitcast.131), calls=%async_computation.27 | async-start | bytes 8388608
  609.1 16.7 %slice-start.4 = ((s8[25165824]{0:T(1024)(128)(4,1)}), s8[4194304]{0:T(1024)(128)(4,1)S(1)}, s32[]{:S(2)}) async-start(s8[25165824]{0:T(1024)(128)(4,1)} %bitcast.131), calls=%async_computation.28 | async-start | bytes 8388608
  609.1 16.7 %slice-start.5 = ((s8[25165824]{0:T(1024)(128)(4,1)}), s8[4194304]{0:T(1024)(128)(4,1)S(1)}, s32[]{:S(2)}) async-start(s8[25165824]{0:T(1024)(128)(4,1)} %bitcast.131), calls=%async_computation.29 | async-start | bytes 8388608
  609.1 16.8 %slice-start.6 = ((s8[25165824]{0:T(1024)(128)(4,1)}), s8[4194304]{0:T(1024)(128)(4,1)S(1)}, s32[]{:S(2)}) async-start(s8[25165824]{0:T(1024)(128)(4,1)} %bitcast.131), calls=%async_computation.30 | async-start | bytes 8388608
  609.1 16.8 %slice-start.7 = ((s8[25165824]{0:T(1024)(128)(4,1)}), s8[4194304]{0:T(1024)(128)(4,1)S(1)}, s32[]{:S(2)}) async-start(s8[25165824]{0:T(1024)(128)(4,1)} %bitcast.131), calls=%async_computation.31 | async-start | bytes 8388608
  819.8 2.7 copy-start.3
  847.9 43.8 %reduce-scatter.7.cloned.1.call-start = ((), (), s32[]{:S(2)}) async-start(), calls=%async_computation.12 | async-start | bytes 14155776 | tf_op jit(solution)/shard_map/reduce_scatter | solution.py:112
  848.5 58.8 %reduce-scatter.9.cloned.1.call-start = ((), (), s32[]{:S(2)}) async-start(), calls=%async_computation.15 | async-start | bytes 14155776 | tf_op jit(solution)/shard_map/reduce_scatter | solution.py:116
  875.4 58.6 %reduce-scatter.11.cloned.1.call-start = ((), (), s32[]{:S(2)}) async-start(), calls=%async_computation.18 | async-start | bytes 14155776 | tf_op jit(solution)/shard_map/reduce_scatter | solution.py:111
  876.1 137.5 %all-gather.20.cloned.1.call-start = ((), (), s32[]{:S(2)}) async-start(), calls=%async_computation.10 | async-start | bytes 14155776 | tf_op jit(solution)/shard_map/all_gather | solution.py:68
  891.7 174.0 %all-gather.24.cloned.1.call-start = ((), (), s32[]{:S(2)}) async-start(), calls=%async_computation.13 | async-start | bytes 14155776 | tf_op jit(solution)/shard_map/all_gather | solution.py:68
  907.3 262.8 %all-gather.28.cloned.1.call-start = ((), (), s32[]{:S(2)}) async-start(), calls=%async_computation.16 | async-start | bytes 14155776 | tf_op jit(solution)/shard_map/all_gather | solution.py:74
  933.9 287.4 %all-gather.32.cloned.1.call-start = ((), (), s32[]{:S(2)}) async-start(), calls=%async_computation.19 | async-start | bytes 14155776 | tf_op jit(solution)/shard_map/all_gather | solution.py:74
  960.4 412.5 %all-reduce.7.cloned.1.call-start = ((), (), s32[]{:S(2)}) async-start(), calls=%async_computation.23 | async-start | bytes 240648192 | tf_op jit(solution)/shard_map/psum | solution.py:119
  961.1 411.8 %all-gather.22.cloned.1.call-start = ((), (), s32[]{:S(2)}) async-start(), calls=%async_computation.11 | async-start | bytes 14155776 | tf_op jit(solution)/shard_map/all_gather | solution.py:70
  1065.7 307.3 %all-gather.26.cloned.1.call-start = ((), (), s32[]{:S(2)}) async-start(), calls=%async_computation.14 | async-start | bytes 14155776 | tf_op jit(solution)/shard_map/all_gather | solution.py:70
  1117.8 269.9 %all-gather.30.cloned.1.call-start = ((), (), s32[]{:S(2)}) async-start(), calls=%async_computation.17 | async-start | bytes 14155776 | tf_op jit(solution)/shard_map/all_gather | solution.py:76
  1221.3 167.4 %all-gather.34.cloned.1.call-start = ((), (), s32[]{:S(2)}) async-start(), calls=%async_computation.20 | async-start | bytes 14155776 | tf_op jit(solution)/shard_map/all_gather | solution.py:76
  1272.4 221.4 %all-reduce.5.cloned.1.call-start = ((), (), s32[]{:S(2)}) async-start(), calls=%async_computation.22 | async-start | bytes 80216064 | tf_op jit(solution)/shard_map/psum | solution.py:122
  1372.9 30.3 %slice-start = ((s8[4718592]{0:T(1024)(128)(4,1)}), s8[524288]{0:T(1024)(128)(4,1)S(1)}, s32[]{:S(2)}) async-start(s8[4718592]{0:T(1024)(128)(4,1)} %bitcast.125), calls=%async_computation.24 | async-start | bytes 1048576
  1388.7 14.5 slice-start.1
  1388.7 14.5 copy-start.1
  1388.7 14.9 copy-start.2
  1406.5 87.3 %copy-start = (f32[768,768]{1,0:T(8,128)S(1)}, f32[768,768]{1,0:T(8,128)}, u32[]{:S(2)}) copy-start(f32[768,768]{1,0:T(8,128)} %get-tuple-element.41) | copy-start | bytes 7077892
Sparse Core Ops, SparseCore 0:
  15.4 162.6 all-gather.35
  180.5 161.7 all-gather.13
  344.6 220.8 all-gather.17
  567.2 222.1 all-gather.15
  848.1 13.8 reduce-scatter.4
  864.7 14.9 reduce-scatter.6
  882.5 14.9 reduce-scatter.8
  900.3 14.9 reduce-scatter.10
  917.4 20.9 all-gather.19
  940.3 20.9 all-gather.23
  963.5 20.9 all-gather.27
  986.4 20.9 all-gather.31
  1010.5 286.8 all-reduce.6
  1299.4 21.0 all-gather.21
  1322.4 20.9 all-gather.25
  1344.8 20.9 all-gather.29
  1367.7 20.9 all-gather.33
  1391.7 102.0 all-reduce.4

commit v2 on v1

v2 whole, which is shorter than its diff:
```python
import functools
import math
import jax
import jax.numpy as jnp
from jax import lax
from jax.experimental import pallas as pl
from jax.experimental.pallas import tpu as pltpu
from jax.sharding import PartitionSpec as P

FACTOR_DECAY = 0.8
GELU_SCALE = math.sqrt(2.0 / math.pi)
GELU_CUBIC = 0.044715
EXACT = lax.Precision.HIGHEST
TN_DIMS = (((0,), (0,)), ((), ()))
NT_DIMS = (((1,), (1,)), ((), ()))


def gelu_value(pre_act):
    tanh_arg = GELU_SCALE * (pre_act + GELU_CUBIC * pre_act * pre_act * pre_act)
    return 0.5 * pre_act * (1.0 + jnp.tanh(tanh_arg))


def gelu_slope(pre_act):
    tanh_arg = GELU_SCALE * (pre_act + GELU_CUBIC * pre_act * pre_act * pre_act)
    tanh_val = jnp.tanh(tanh_arg)
    return 0.5 * (1.0 + tanh_val) + 0.5 * pre_act * (1.0 - tanh_val * tanh_val) * GELU_SCALE * (1.0 + 3.0 * GELU_CUBIC * pre_act * pre_act)


def activate(pre_act):
    return gelu_value(pre_act.astype(jnp.float32)).astype(jnp.bfloat16)


def back_gate(grad_act, pre_act):
    return (grad_act.astype(jnp.float32) * gelu_slope(pre_act.astype(jnp.float32))).astype(jnp.bfloat16)


def matmul(left_mat, right_mat):
    return jnp.dot(left_mat, right_mat, preferred_element_type=jnp.float32)


def matmul_tn(left_mat, right_mat):
    return lax.dot_general(left_mat, right_mat, TN_DIMS, preferred_element_type=jnp.float32)


def matmul_nt(left_mat, right_mat):
    return lax.dot_general(left_mat, right_mat, NT_DIMS, preferred_element_type=jnp.float32)


def exact_dot(left_mat, right_mat):
    return jnp.dot(left_mat, right_mat, precision=EXACT, preferred_element_type=jnp.float32)


SWAP = [(0, 1), (1, 0)]
BLEND_ROWS = 256


def blend_blocks(old_mats, first_pair, second_pair, inv_rows):
    return FACTOR_DECAY * old_mats + (1.0 - FACTOR_DECAY) * inv_rows * jnp.stack([sum(first_pair), sum(second_pair)])


def blend_kernel(term_count, scale, old_ref, *refs):
    total = refs[0][...]
    for term in range(1, term_count):
        total = total + refs[term][...]
    refs[-1][0] = FACTOR_DECAY * old_ref[0] + scale * total


def blend_layer(old_mats, terms, layer, inv_rows, written=None):
    dim = old_mats.shape[1]
    stacked = pl.BlockSpec((1, BLEND_ROWS, dim), lambda row: (layer, row, 0))
    plain = pl.BlockSpec((BLEND_ROWS, dim), lambda row: (row, 0))
    operands = [old_mats, *terms]
    in_specs = [stacked] + [plain] * len(terms)
    aliases = {}
    if written is not None:
        aliases = {len(operands): 0}
        operands.append(written)
        in_specs.append(pl.BlockSpec(memory_space=pl.ANY))
    return pl.pallas_call(
        functools.partial(blend_kernel, len(terms), (1.0 - FACTOR_DECAY) * inv_rows),
        out_shape=jax.ShapeDtypeStruct(old_mats.shape, jnp.float32),
        grid=(dim // BLEND_ROWS,),
        in_specs=in_specs,
        out_specs=stacked,
        input_output_aliases=aliases,
        cost_estimate=pl.CostEstimate(flops=10 ** 10, bytes_accessed=4 * dim * dim * (2 + len(terms)), transcendentals=0),
        compiler_params=pltpu.CompilerParams(vmem_limit_bytes=40 * 2 ** 20),
        name="blend_layer",
    )(*operands)


def solution(mesh):
    data_ways = mesh.shape['data']
    model_ways = mesh.shape['model']

    def to_rows(col_part):
        return lax.all_to_all(col_part, 'model', split_axis=0, concat_axis=1, tiled=True)

    def gather_weight(part):
        return lax.all_gather(core_half(part, 0, 0), ('model', 'data'), axis=0, tiled=True)

    def core_half(full, axis, shift):
        half = full.shape[axis] // data_ways
        core = (lax.axis_index('data') + shift) % data_ways
        return lax.dynamic_slice_in_dim(full, core * half, half, axis)

    def swap_cores(part):
        return lax.ppermute(part, 'data', SWAP)

    def pair_scatter(full, axis):
        return core_half(full, axis, 0) + swap_cores(core_half(full, axis, 1))

    def pair_gather(part, axis):
        other = swap_cores(part)
        return jnp.where(lax.axis_index('data') == 0, jnp.concatenate([part, other], axis), jnp.concatenate([other, part], axis))

    def own_gram(acts):
        width = acts.shape[1] // model_ways
        return matmul_tn(lax.dynamic_slice_in_dim(acts, lax.axis_index('model') * width, width, 1), acts)

    def whole_gram(part):
        part = lax.psum_scatter(part, 'data', scatter_dimension=0, tiled=True)
        return lax.all_gather(part, ('model', 'data'), axis=0, tiled=True)

    def layer_half(mats, layer, axis):
        half = mats.shape[axis] // data_ways
        starts = [layer, 0, 0]
        sizes = [1, mats.shape[1], mats.shape[2]]
        starts[axis] = lax.axis_index('data') * half
        sizes[axis] = half
        return lax.dynamic_slice(mats, starts, sizes).reshape(sizes[1:])

    def shard_body(x_tokens, dy_tokens, w_col, w_row, a_old_col, s_old_col, a_old_row, s_old_row, a_inv_col, s_inv_col, a_inv_row, s_inv_row):
        inv_rows = 1.0 / (x_tokens.shape[0] * data_ways)
        w_two = gather_weight(w_row[0])
        w_three_t = gather_weight(w_col[1].T)
        z_one = matmul(x_tokens, w_col[0]).astype(jnp.bfloat16)
        h_one = activate(z_one)
        h_one_t = to_rows(h_one)
        dh_three = matmul_nt(dy_tokens, w_row[1]).astype(jnp.bfloat16)
        a_one = matmul_tn(x_tokens, x_tokens)
        h_one_t, dh_three, a_one = lax.optimization_barrier((h_one_t, dh_three, a_one))
        dh_three_t = to_rows(dh_three)
        a_one_pair = swap_cores(a_one)
        z_two_t = matmul(h_one_t, w_two).astype(jnp.bfloat16)
        h_two_t = activate(z_two_t)
        h_two = lax.all_gather(h_two_t, 'model', axis=0, tiled=True)
        s_four = matmul_tn(dy_tokens, dy_tokens)
        a_one_rows = layer_half(a_inv_col, 0, 1)
        a_three_rows = layer_half(a_inv_col, 1, 1)
        s_two_cols = layer_half(s_inv_row, 0, 2)
        s_four_cols = layer_half(s_inv_row, 1, 2)
        (dh_three_t, s_four, a_one_rows, a_three_rows, s_two_cols, s_four_cols) = lax.optimization_barrier(
            (dh_three_t, s_four, a_one_rows, a_three_rows, s_two_cols, s_four_cols))
        s_four_pair = swap_cores(s_four)
        a_two = matmul_tn(h_one, h_one)
        z_three_t = matmul_nt(h_two_t, w_three_t).astype(jnp.bfloat16)
        g_three_t = back_gate(dh_three_t, z_three_t)
        dh_two_t = matmul(g_three_t, w_three_t).astype(jnp.bfloat16)
        g_two_t = back_gate(dh_two_t, z_two_t)
        g_two = lax.all_gather(g_two_t, 'model', axis=0, tiled=True)
        a_new_part = blend_layer(a_old_col, [a_one, a_one_pair], 0, inv_rows)
        s_new_part = blend_layer(s_old_row, [s_four, s_four_pair], 1, inv_rows)
        h_two, a_two, g_two_t, a_new_part, s_new_part = lax.optimization_barrier(
            (h_two, a_two, g_two_t, a_new_part, s_new_part))

        z_three = matmul(h_two, w_col[1]).astype(jnp.bfloat16)
        h_three = activate(z_three)
        g_three = back_gate(dh_three, z_three)
        grad_four = pair_scatter(matmul_tn(h_three, dy_tokens), 1) * inv_rows
        grad_three = pair_scatter(matmul_tn(h_two, g_three), 0) * inv_rows
        a_three = own_gram(h_two)
        a_four = matmul_tn(h_three, h_three)
        s_three = matmul_tn(g_three, g_three)
        left_four = pair_gather(exact_dot(a_inv_row[1], grad_four), 1)
        right_three = pair_gather(exact_dot(grad_three, s_inv_col[1]), 0)
        g_two, left_four, right_three, a_two, a_three, a_four, s_three = lax.optimization_barrier(
            (g_two, left_four, right_three, a_two, a_three, a_four, s_three))

        g_one = back_gate(matmul_nt(g_two, w_row[0]).astype(jnp.bfloat16), z_one)
        grad_one = lax.psum_scatter(matmul_tn(x_tokens, g_one), 'data', scatter_dimension=0, tiled=True) * inv_rows
        grad_two = lax.psum_scatter(matmul_tn(h_one, g_two), 'data', scatter_dimension=1, tiled=True) * inv_rows
        s_two = own_gram(g_two)
        s_one = matmul_tn(g_one, g_one)
        right_one = lax.all_gather(exact_dot(grad_one, s_inv_col[0]), 'data', axis=0, tiled=True)
        left_two = lax.all_gather(exact_dot(a_inv_row[0], grad_two), 'data', axis=1, tiled=True)
        right_one, left_two, a_three, s_two = lax.optimization_barrier((right_one, left_two, a_three, s_two))
        a_three = whole_gram(a_three)
        s_two = whole_gram(s_two)

        u_three = pair_gather(exact_dot(a_three_rows, right_three), 0)
        u_four = pair_gather(exact_dot(left_four, s_four_cols), 1)
        u_one = pair_gather(exact_dot(a_one_rows, right_one), 0)
        u_two = pair_gather(exact_dot(left_two, s_two_cols), 1)
        u_col = jnp.stack([u_one, u_three])
        u_row = jnp.stack([u_two, u_four])
        s_new_col = blend_blocks(s_old_col, (s_one, swap_cores(s_one)), (s_three, swap_cores(s_three)), inv_rows)
        a_new_row = blend_blocks(a_old_row, (a_two, swap_cores(a_two)), (a_four, swap_cores(a_four)), inv_rows)
        a_new_col = blend_layer(a_old_col, [a_three], 1, inv_rows, a_new_part)
        s_new_row = blend_layer(s_old_row, [s_two], 0, inv_rows, s_new_part)
        return (u_col, u_row, a_new_col, s_new_col, a_new_row, s_new_row)

    batch_split = P('data', None)
    col_split = P(None, None, 'model')
    row_split = P(None, 'model', None)
    replicated = P()
    return jax.shard_map(
        shard_body,
        mesh=mesh,
        in_specs=(batch_split, batch_split, col_split, row_split, replicated, row_split, row_split, replicated, replicated, row_split, row_split, replicated),
        out_specs=(col_split, row_split, replicated, row_split, row_split, replicated),
        check_vma=False,
    )
```

time: 1590 us -> 1380 us (0.87)
  Pallas kernels: 0 us -> 170 us
  matrix products: 1030 us -> 908 us
  blocking collectives: 119 us -> 0 us
  other arithmetic: 191 us -> 89.4 us
  local copies, waits for them, and re-layouts: 143 us -> 94 us
    pallas_call x0 -> x4, Pallas kernels: none -> 170 us  [blend_layer(): pl.pallas_call(functools.partial(blend_kernel, len(terms), (1.0 - FACTOR_...]
    add x4 -> x2, other arithmetic: 153 us -> 5.89 us  [blend_blocks(): FACTOR_DECAY * old_mats]
    dot_general x12, matrix products: 509 us -> 385 us  [matmul_tn(): lax.dot_general(left_mat, right_mat, TN_DIMS, preferred_element_type=jnp....]
    all_to_all x1 -> x0, blocking collectives: 119 us -> none  [to_rows(): lax.all_to_all(col_part, 'model', split_axis=0, concat_axis=1, tiled=True)]
    slice x2 -> x0, local copies, waits for them, and re-layouts: 105 us -> none  [the longest x1 52.5 us: shard_body(): a_inv_col[0]]
    select_n x0 -> x6, other arithmetic: none -> 55.4 us  [pair_gather(): jnp.where(lax.axis_index('data') == 0, jnp.concatenate([part, other], axi...]
    reshape x0 -> x2, local copies, waits for them, and re-layouts: none -> 53 us  [layer_half(): return lax.dynamic_slice(mats, starts, sizes).reshape(sizes[1:])]
    reduce_scatter x2, waiting for transfers between devices: 0.04 us -> 30.1 us  [whole_gram(): part = lax.psum_scatter(part, 'data', scatter_dimension=0, tiled=True)]
  transfers between devices with their start and end apart: 19 -> 28, of which waited for: 6 -> 5; matrix products, arithmetic and copies ran while one was open for 77% -> 74% of each run, Pallas kernels for 0% -> 10%
where the time goes in v2:
time: 1380 us; the launch traced here: 1370 us
  matrix products  908 us (66%)
  Pallas kernels  170 us (12%)
  local copies, waits for them, and re-layouts  94 us (7%)
  other arithmetic  89.4 us (6%)
  waiting for transfers between devices  84.3 us (6%)
  between operations  15 us (1%)
  starting transfers between devices  14.5 us (1%)
    dot_general x12, matrix products, matmul_tn(): lax.dot_general(left_mat, right_mat, TN_DIMS, preferred_element_type=jnp....  385 us
    dot_general x8, matrix products, exact_dot(): jnp.dot(left_mat, right_mat, precision=EXACT, preferred_element_type=jnp....  292 us
    pallas_call x4, Pallas kernels, blend_layer(): pl.pallas_call(functools.partial(blend_kernel, len(terms), (1.0 - FACTOR_...  170 us
    dot_general x4, matrix products, matmul(): return jnp.dot(left_mat, right_mat, preferred_element_type=jnp.float32)  139 us
    dot_general x3, matrix products, matmul_nt(): lax.dot_general(left_mat, right_mat, NT_DIMS, preferred_element_type=jnp....  92.4 us
    select_n x6, other arithmetic, pair_gather(): jnp.where(lax.axis_index('data') == 0, jnp.concatenate([part, other], axi...  55.4 us
    reshape x2, local copies, waits for them, and re-layouts, layer_half(): return lax.dynamic_slice(mats, starts, sizes).reshape(sizes[1:])  53 us
    all_gather x2, waiting for transfers between devices, whole_gram(): return lax.all_gather(part, ('model', 'data'), axis=0, tiled=True)  31.5 us
  transfers between devices with their start and end apart: 28, of which 5 were waited for; matrix products, arithmetic and copies ran while one was open for 74% of the time, Pallas kernels for 10%

profile of v2, /device:TPU:0, one launch (start us, length us, event | category | flops | bytes accessed | tf_op | source)
XLA Modules:
  0.0 1374.9 jit_solution(7544396751319333374)
XLA Ops:
  19.4 29.7 %fusion.20 = (bf16[4096,768]{1,0:T(8,128)(2,1)}, bf16[4096,768]{1,0:T(8,128)(2,1)}) fusion(bf16[4096,3072]{1,0:T(8,128)(2,1)} %param.12, bf16[2,3072,768]{2,1,0:T(8,128)(2,1)} %param.14), kind=kOutput, calls=%fused_computation.54 | convolution fusion | flops 19361955840 | bytes 42467328 | tf_op jit(solution)/shard_map/dot_general | solution.py:38
  63.3 90.1 %fusion.120.refs_0_ = f32[3072,3072]{1,0:T(8,128)} fusion(bf16[4096,3072]{1,0:T(8,128)(2,1)} %param.12), kind=kOutput, calls=%fused_computation.163 | convolution fusion | flops 77309411328 | bytes 62914560 | tf_op jit(solution)/shard_map/dot_general | solution.py:42
  153.4 25.6 %convolution_convert_fusion.2 = bf16[4096,768]{1,0:T(8,128)(2,1)} fusion(bf16[4096,3072]{1,0:T(8,128)(2,1)} %param.13, bf16[2,768,3072]{2,1,0:T(8,128)(2,1)} %param.15), kind=kOutput, calls=%fused_computation.86 | convolution fusion | flops 19330498560 | bytes 36175872 | tf_op jit(solution)/shard_map/dot_general | solution.py:46
  184.4 29.3 %fusion.14 = (bf16[1024,3072]{1,0:T(8,128)(2,1)}, bf16[1024,3072]{1,0:T(8,128)(2,1)}) fusion(bf16[1024,3072]{0,1:T(8,128)(2,1)} %bitcast.3, bf16[1,3072,3072]{2,1,0:T(8,128)(2,1)} %all-gather.24.cloned.1.call-done), kind=kOutput, calls=%fused_computation.48 | convolution fusion | flops 19361955840 | bytes 37748736 | tf_op jit(solution)/shard_map/dot_general | solution.py:38
  213.7 90.0 %fusion.121.refs_0_ = f32[3072,3072]{1,0:T(8,128)} fusion(bf16[4096,3072]{1,0:T(8,128)(2,1)} %param.13), kind=kOutput, calls=%fused_computation.164 | convolution fusion | flops 77309411328 | bytes 62914560 | tf_op jit(solution)/shard_map/dot_general | solution.py:42
  303.7 26.7 %dynamic-slice_bitcast_fusion.2 = (f32[1536,3072]{1,0:T(8,128)}, f32[1536,3072]{1,0:T(8,128)}) fusion(f32[2,3072,3072]{2,1,0:T(8,128)} %param.20, s32[]{:T(128)S(6)} %select_n.106), kind=kLoop, calls=%fused_computation.34 | loop fusion | bytes 75497472 | tf_op jit(solution)/shard_map/reshape | solution.py:131
  330.6 26.4 %dynamic-slice_bitcast_fusion = (f32[3072,1536]{1,0:T(8,128)}, f32[3072,1536]{1,0:T(8,128)}) fusion(f32[2,3072,3072]{2,1,0:T(8,128)} %param.23, s32[]{:T(128)S(6)} %select_n.106), kind=kLoop, calls=%fused_computation.32 | loop fusion | bytes 75497472 | tf_op jit(solution)/shard_map/reshape | solution.py:131
  363.5 36.3 %fusion.118 = bf16[1024,3072]{1,0:T(8,128)(2,1)} fusion(bf16[3072,3072]{0,1:T(8,128)(2,1)} %all-gather.10.cloned.1.call-done, bf16[1024,3072]{1,0:T(8,128)(2,1)} %get-tuple-element.61), kind=kOutput, calls=%fused_computation.162 | convolution fusion | flops 19358810112 | bytes 31457280 | tf_op jit(solution)/shard_map/dot_general | solution.py:46
  399.8 45.7 %fusion.19 = bf16[1024,3072]{1,0:T(8,128)(2,1)} fusion(bf16[1024,3072]{1,0:T(8,128)(2,1)} %get-tuple-element.61, bf16[3072,3072]{0,1:T(8,128)(2,1)} %all-gather.10.cloned.1.call-done, bf16[1024,3072]{1,0:T(8,128)(2,1)} %bitcast.119, bf16[1024,3072]{1,0:T(8,128)(2,1)} %fusion.118), kind=kOutput, calls=%fused_computation.53 | convolution fusion | flops 19462619136 | bytes 44040192 | tf_op jit(solution)/shard_map/dot_general | solution.py:38
  456.1 48.3 %blend_layer.4.refs_1_ = f32[2,3072,3072]{2,1,0:T(8,128)} custom-call(f32[2,3072,3072]{2,1,0:T(8,128)} %old_ref.6, f32[3072,3072]{1,0:T(8,128)} %fusion.120.refs_0_, f32[3072,3072]{1,0:T(8,128)} %collective-permute-done.refs_1_), custom_call_target="tpu_custom_call" | custom-call | flops 10000000000 | bytes 150994944 | tf_op jit(solution)/shard_map/blend_layer/pallas_call | solution.py:79
  504.3 48.3 %blend_layer.5.refs_1_ = f32[2,3072,3072]{2,1,0:T(8,128)} custom-call(f32[2,3072,3072]{2,1,0:T(8,128)} %old_ref.7, f32[3072,3072]{1,0:T(8,128)} %fusion.121.refs_0_, f32[3072,3072]{1,0:T(8,128)} %collective-permute-done.1.refs_1_), custom_call_target="tpu_custom_call" | custom-call | flops 10000000000 | bytes 150994944 | tf_op jit(solution)/shard_map/blend_layer/pallas_call | solution.py:79
  566.5 34.1 %fusion.13 = (bf16[4096,768]{1,0:T(8,128)(2,1)S(1)}, bf16[4096,768]{1,0:T(8,128)(2,1)}) fusion(bf16[4096,768]{1,0:T(8,128)(2,1)} %convolution_convert_fusion.2, bf16[4096,3072]{1,0:T(8,128)(2,1)} %all-gather.14.cloned.1.call-done, bf16[2,3072,768]{2,1,0:T(8,128)(2,1)} %param.14), kind=kOutput, calls=%fused_computation.47 | convolution fusion | flops 19396558848 | bytes 48758784 | tf_op jit(solution)/shard_map/dot_general | solution.py:38
  600.6 34.3 %fusion.114 = f32[768,3072]{1,0:T(8,128)S(1)} fusion(bf16[4096,3072]{1,0:T(8,128)(2,1)} %param.13, bf16[4096,768]{1,0:T(8,128)(2,1)} %get-tuple-element.63), kind=kOutput, calls=%fused_computation.159 | convolution fusion | flops 19358810112 | bytes 40894464 | tf_op jit(solution)/shard_map/dot_general | solution.py:42
  640.1 24.3 %fusion.123 = f32[3072,768]{1,0:T(8,128)S(1)} fusion(bf16[4096,3072]{1,0:T(8,128)(2,1)} %all-gather.14.cloned.1.call-done, bf16[4096,768]{1,0:T(8,128)(2,1)S(1)} %get-tuple-element.62), kind=kOutput, calls=%fused_computation.166 | convolution fusion | flops 19327352832 | bytes 40894464 | tf_op jit(solution)/shard_map/dot_general | solution.py:42
  670.6 27.0 %fusion.81 = f32[768,1536]{0,1:T(8,128)} fusion(f32[768,1536]{1,0:T(8,128)} %collective-permute-done.2, f32[768,3072]{1,0:T(8,128)} %copy-done.1, s32[]{:T(128)S(6)} %select_n.110, f32[2,768,768]{2,1,0:T(8,128)} %param.22), kind=kOutput, calls=%fused_computation.123 | convolution fusion | flops 10873995264 | bytes 16515076 | tf_op jit(solution)/shard_map/dot_general | solution.py:50
  698.2 15.7 %fusion.71 = f32[1536,768]{1,0:T(8,128)} fusion(f32[1536,768]{1,0:T(8,128)} %collective-permute-done.4, f32[3072,768]{1,0:T(8,128)S(1)} %bitcast.116, s32[]{:T(128)S(6)} %select_n.110, f32[2,768,768]{2,1,0:T(8,128)} %param.21), kind=kOutput, calls=%fused_computation.113 | convolution fusion | flops 10873995264 | bytes 16515076 | tf_op jit(solution)/shard_map/dot_general | solution.py:50
  720.6 16.4 %fusion.112 = f32[768,768]{1,0:T(8,128)} fusion(bf16[4096,768]{1,0:T(8,128)(2,1)} %get-tuple-element.63), kind=kOutput, calls=%fused_computation.158 | convolution fusion | flops 4863295488 | bytes 8650752 | tf_op jit(solution)/shard_map/dot_general | solution.py:42
  737.1 22.6 %fusion.48 = f32[768,3072]{1,0:T(8,128)} fusion(bf16[4096,3072]{1,0:T(8,128)(2,1)S(1)} %bitcast.128, s32[]{:T(128)S(6)} %select_n.116), kind=kOutput, calls=%fused_computation.91 | convolution fusion | flops 19327352832 | bytes 40894468 | tf_op jit(solution)/shard_map/dot_general | solution.py:42
  790.3 30.5 %fusion.25 = bf16[4096,768]{1,0:T(8,128)(2,1)S(1)} fusion(bf16[4096,768]{1,0:T(8,128)(2,1)} %get-tuple-element.59, bf16[4096,3072]{1,0:T(8,128)(2,1)} %all-gather.12.cloned.1.call-done, bf16[2,768,3072]{2,1,0:T(8,128)(2,1)} %param.15), kind=kOutput, calls=%fused_computation.59 | convolution fusion | flops 19396558848 | bytes 42467328 | tf_op jit(solution)/shard_map/dot_general | solution.py:46
  823.5 25.3 %convolution_bitcast_fusion = f32[3072,768]{1,0:T(8,128)} fusion(bf16[4096,768]{1,0:T(8,128)(2,1)S(1)} %fusion.25, bf16[4096,3072]{1,0:T(8,128)(2,1)} %param.12), kind=kOutput, calls=%fused_computation.100 | convolution fusion | flops 19327352832 | bytes 40894464 | tf_op jit(solution)/shard_map/dot_general | solution.py:42
  848.8 26.8 %fusion.125 = f32[768,3072]{1,0:T(8,128)} fusion(bf16[4096,768]{1,0:T(8,128)(2,1)} %get-tuple-element.58, bf16[4096,3072]{1,0:T(8,128)(2,1)} %all-gather.12.cloned.1.call-done), kind=kOutput, calls=%fused_computation.168 | convolution fusion | flops 19327352832 | bytes 40894464 | tf_op jit(solution)/shard_map/dot_general | solution.py:42
  875.7 15.5 %fusion.69 = f32[1536,768]{1,0:T(8,128)} fusion(f32[1536,768]{1,0:T(8,128)} %reduce-scatter.5.cloned.1.call-done, f32[2,768,768]{2,1,0:T(8,128)} %param.21), kind=kOutput, calls=%fused_computation.111 | convolution fusion | flops 10872815616 | bytes 11796480 | tf_op jit(solution)/shard_map/dot_general | solution.py:50
  891.3 26.4 %fusion.84 = f32[768,1536]{0,1:T(8,128)} fusion(f32[768,1536]{1,0:T(8,128)} %reduce-scatter.7.cloned.1.call-done, f32[2,768,768]{2,1,0:T(8,128)} %param.22), kind=kOutput, calls=%fused_computation.124 | convolution fusion | flops 10872815616 | bytes 11796480 | tf_op jit(solution)/shard_map/dot_general | solution.py:50
  917.7 27.4 %fusion.46 = f32[768,3072]{1,0:T(8,128)} fusion(bf16[4096,3072]{1,0:T(8,128)(2,1)} %all-gather.12.cloned.1.call-done, s32[]{:T(128)S(6)} %select_n.116), kind=kOutput, calls=%fused_computation.89 | convolution fusion | flops 19327352832 | bytes 40894468 | tf_op jit(solution)/shard_map/dot_general | solution.py:42
  958.9 17.1 %reduce-scatter.11.cloned.1.call-done = f32[384,3072]{1,0:T(8,128)} async-done(((f32[768,3072]{1,0:T(8,128)}), f32[384,3072]{1,0:T(8,128)}) %reduce-scatter.11.cloned.1.call-update) | async-done | bytes 4718608 | tf_op jit(solution)/shard_map/reduce_scatter | solution.py:122
  976.1 52.1 %fusion.127 = f32[1536,768]{1,0:T(8,128)} fusion(f32[1536,3072]{1,0:T(8,128)} %get-tuple-element.41, f32[3072,768]{1,0:T(8,128)} %maximum_select_fusion.1), kind=kOutput, calls=%fused_computation.170 | convolution fusion | flops 43486543872 | bytes 33030144 | tf_op jit(solution)/shard_map/dot_general | solution.py:50
  1028.3 50.0 %fusion.129 = f32[768,1536]{1,0:T(8,128)} fusion(f32[768,3072]{0,1:T(8,128)} %maximum_select_fusion, f32[3072,1536]{1,0:T(8,128)S(1)} %bitcast.114), kind=kOutput, calls=%fused_computation.172 | convolution fusion | flops 43486543872 | bytes 33030144 | tf_op jit(solution)/shard_map/dot_general | solution.py:50
  1089.6 54.4 %fusion.126 = f32[1536,768]{1,0:T(8,128)S(1)} fusion(f32[1536,3072]{1,0:T(8,128)} %get-tuple-element.31, f32[3072,768]{1,0:T(8,128)} %all-gather.16.cloned.1.call-done), kind=kOutput, calls=%fused_computation.169 | convolution fusion | flops 43486543872 | bytes 33030144 | tf_op jit(solution)/shard_map/dot_general | solution.py:50
  1144.6 51.1 %fusion.128 = f32[768,1536]{1,0:T(8,128)} fusion(f32[768,3072]{0,1:T(8,128)} %all-gather.18.cloned.1.call-done, f32[3072,1536]{1,0:T(8,128)S(1)} %bitcast.112), kind=kOutput, calls=%fused_computation.171 | convolution fusion | flops 43486543872 | bytes 33030144 | tf_op jit(solution)/shard_map/dot_general | solution.py:50
  1263.1 36.6 %blend_layer.6 = f32[2,3072,3072]{2,1,0:T(8,128)} custom-call(f32[2,3072,3072]{2,1,0:T(8,128)} %old_ref.6, f32[3072,3072]{1,0:T(8,128)} %all-gather.20.cloned.1.call-done.refs_0_, f32[2,3072,3072]{2,1,0:T(8,128)} %blend_layer.4.refs_1_), custom_call_target="tpu_custom_call", output_to_operand_aliasing={{}: (2, {})} | custom-call | flops 10000000000 | bytes 113246208 | tf_op jit(solution)/shard_map/blend_layer/pallas_call | solution.py:79
  1299.7 31.5 %all-gather.22.cloned.1.call-done.refs_0_ = f32[3072,3072]{1,0:T(8,128)} async-done(((f32[384,3072]{1,0:T(8,128)}), f32[3072,3072]{1,0:T(8,128)}) %all-gather.22.cloned.1.call-update) | async-done | bytes 37748752 | tf_op jit(solution)/shard_map/all_gather | solution.py:123
  1331.2 36.6 %blend_layer.7 = f32[2,3072,3072]{2,1,0:T(8,128)} custom-call(f32[2,3072,3072]{2,1,0:T(8,128)} %old_ref.7, f32[3072,3072]{1,0:T(8,128)} %all-gather.22.cloned.1.call-done.refs_0_, f32[2,3072,3072]{2,1,0:T(8,128)} %blend_layer.5.refs_1_), custom_call_target="tpu_custom_call", output_to_operand_aliasing={{}: (2, {})} | custom-call | flops 10000000000 | bytes 113246208 | tf_op jit(solution)/shard_map/blend_layer/pallas_call | solution.py:79
  (161 shorter events, 207.8 us)
Async XLA Ops:
  7.2 177.2 %all-gather.24.cloned.1.call-start = ((), (), s32[]{:S(2)}) async-start(), calls=%async_computation.17 | async-start | bytes 21233664 | tf_op jit(solution)/shard_map/all_gather | solution.py:100
  15.3 348.2 %all-gather.10.cloned.1.call-start = ((), (), s32[]{:S(2)}) async-start(), calls=%async_computation.6 | async-start | bytes 21233664 | tf_op jit(solution)/shard_map/all_gather | solution.py:100
  57.7 121.4 %all-to-all-start = ((bf16[4,1024,768]{1,2,0:T(8,128)(2,1)}), bf16[4,1024,768]{1,2,0:T(8,128)(2,1)}, u32[]{:S(2)}, u32[]{:S(2)}) async-start(bf16[4,1024,768]{1,2,0:T(8,128)(2,1)} %copy.21), calls=%async_computation | async-start | bytes 12582912 | tf_op jit(solution)/shard_map/all_to_all | solution.py:97
  179.1 177.9 %all-to-all-start.1 = ((bf16[4,1024,768]{2,1,0:T(8,128)(2,1)}), bf16[4,1024,768]{2,1,0:T(8,128)(2,1)}, u32[]{:S(2)}, u32[]{:S(2)}) async-start(bf16[4,1024,768]{2,1,0:T(8,128)(2,1)} %bitcast.118), calls=%async_computation.1 | async-start | bytes 12582912 | tf_op jit(solution)/shard_map/all_to_all | solution.py:97
  184.3 382.2 %all-gather.14.cloned.1.call-start = ((), (), s32[]{:S(2)}) async-start(), calls=%async_computation.8 | async-start | bytes 31457280 | tf_op jit(solution)/shard_map/all_gather | solution.py:147
  213.7 576.6 %all-gather.12.cloned.1.call-start = ((), (), s32[]{:S(2)}) async-start(), calls=%async_computation.7 | async-start | bytes 31457280 | tf_op jit(solution)/shard_map/all_gather | solution.py:161
  330.4 125.6 %collective-permute-start = (f32[3072,3072]{1,0:T(8,128)}, f32[3072,3072]{1,0:T(8,128)}, u32[]{:S(2)}, u32[]{:S(2)}) collective-permute-start(f32[3072,3072]{1,0:T(8,128)} %fusion.120.refs_0_), channel_id=1, source_target_pairs={{0,1},{1,0},{2,3},{3,2},{4,5},{5,4},{6,7},{7,6}} | collective-permute-start | bytes 113246216 | tf_op jit(solution)/shard_map/ppermute | solution.py:108
  363.2 141.1 %collective-permute-start.1 = (f32[3072,3072]{1,0:T(8,128)}, f32[3072,3072]{1,0:T(8,128)}, u32[]{:S(2)}, u32[]{:S(2)}) collective-permute-start(f32[3072,3072]{1,0:T(8,128)} %fusion.121.refs_0_), channel_id=1, source_target_pairs={{0,1},{1,0},{2,3},{3,2},{4,5},{5,4},{6,7},{7,6}} | collective-permute-start | bytes 113246216 | tf_op jit(solution)/shard_map/ppermute | solution.py:108
  445.5 430.2 %reduce-scatter.5.cloned.1.call-start = ((), (), s32[]{:S(2)}) async-start(), calls=%async_computation.9 | async-start | bytes 14155776 | tf_op jit(solution)/shard_map/reduce_scatter | solution.py:181
  637.9 32.7 %collective-permute-start.2 = (f32[768,1536]{1,0:T(8,128)}, f32[768,1536]{1,0:T(8,128)}, u32[]{:S(2)}, u32[]{:S(2)}) collective-permute-start(f32[768,1536]{1,0:T(8,128)} %constant_dynamic-slice_fusion.1), channel_id=1, source_target_pairs={{0,1},{1,0},{2,3},{3,2},{4,5},{5,4},{6,7},{7,6}} | collective-permute-start | bytes 14155784 | tf_op jit(solution)/shard_map/ppermute | solution.py:108
  670.6 27.6 %collective-permute-start.4 = (f32[1536,768]{1,0:T(8,128)}, f32[1536,768]{1,0:T(8,128)}, u32[]{:S(2)}, u32[]{:S(2)}) collective-permute-start(f32[1536,768]{1,0:T(8,128)} %constant_dynamic-slice_fusion), channel_id=1, source_target_pairs={{0,1},{1,0},{2,3},{3,2},{4,5},{5,4},{6,7},{7,6}} | collective-permute-start | bytes 14155784 | tf_op jit(solution)/shard_map/ppermute | solution.py:108
  697.6 62.1 %collective-permute-start.3 = (f32[768,1536]{0,1:T(8,128)}, f32[768,1536]{0,1:T(8,128)}, u32[]{:S(2)}, u32[]{:S(2)}) collective-permute-start(f32[768,1536]{0,1:T(8,128)} %fusion.81), channel_id=1, source_target_pairs={{0,1},{1,0},{2,3},{3,2},{4,5},{5,4},{6,7},{7,6}} | collective-permute-start | bytes 14155784 | tf_op jit(solution)/shard_map/ppermute | solution.py:108
  713.9 57.4 %collective-permute-start.5 = (f32[1536,768]{1,0:T(8,128)}, f32[1536,768]{1,0:T(8,128)}, u32[]{:S(2)}, u32[]{:S(2)}) collective-permute-start(f32[1536,768]{1,0:T(8,128)} %fusion.71), channel_id=1, source_target_pairs={{0,1},{1,0},{2,3},{3,2},{4,5},{5,4},{6,7},{7,6}} | collective-permute-start | bytes 14155784 | tf_op jit(solution)/shard_map/ppermute | solution.py:108
  848.8 42.5 %reduce-scatter.7.cloned.1.call-start = ((), (), s32[]{:S(2)}) async-start(), calls=%async_computation.11 | async-start | bytes 14155776 | tf_op jit(solution)/shard_map/reduce_scatter | solution.py:182
  875.7 69.5 %all-gather.16.cloned.1.call-start = ((), (), s32[]{:S(2)}) async-start(), calls=%async_computation.10 | async-start | bytes 14155776 | tf_op jit(solution)/shard_map/all_gather | solution.py:185
  891.2 53.9 %all-gather.18.cloned.1.call-start = ((), (), s32[]{:S(2)}) async-start(), calls=%async_computation.12 | async-start | bytes 14155776 | tf_op jit(solution)/shard_map/all_gather | solution.py:186
  917.7 41.2 %reduce-scatter.9.cloned.1.call-start = ((), (), s32[]{:S(2)}) async-start(), calls=%async_computation.13 | async-start | bytes 14155776 | tf_op jit(solution)/shard_map/reduce_scatter | solution.py:122
  945.2 30.8 %reduce-scatter.11.cloned.1.call-start = ((), (), s32[]{:S(2)}) async-start(), calls=%async_computation.15 | async-start | bytes 14155776 | tf_op jit(solution)/shard_map/reduce_scatter | solution.py:122
  945.8 317.3 %all-gather.20.cloned.1.call-start = ((), (), s32[]{:S(2)}) async-start(), calls=%async_computation.14 | async-start | bytes 42467328 | tf_op jit(solution)/shard_map/all_gather | solution.py:123
  958.9 372.3 %all-gather.22.cloned.1.call-start = ((), (), s32[]{:S(2)}) async-start(), calls=%async_computation.16 | async-start | bytes 42467328 | tf_op jit(solution)/shard_map/all_gather | solution.py:123
  1028.2 184.6 %collective-permute-start.7 = (f32[1536,768]{1,0:T(8,128)}, f32[1536,768]{1,0:T(8,128)}, u32[]{:S(2)}, u32[]{:S(2)}) collective-permute-start(f32[1536,768]{1,0:T(8,128)} %fusion.127), channel_id=1, source_target_pairs={{0,1},{1,0},{2,3},{3,2},{4,5},{5,4},{6,7},{7,6}} | collective-permute-start | bytes 14155784 | tf_op jit(solution)/shard_map/ppermute | solution.py:108
  1078.4 141.9 %collective-permute-start.9 = (f32[768,1536]{1,0:T(8,128)}, f32[768,1536]{1,0:T(8,128)S(1)}, u32[]{:S(2)}, u32[]{:S(2)}) collective-permute-start(f32[768,1536]{1,0:T(8,128)} %fusion.129), channel_id=1, source_target_pairs={{0,1},{1,0},{2,3},{3,2},{4,5},{5,4},{6,7},{7,6}} | collective-permute-start | bytes 14155784 | tf_op jit(solution)/shard_map/ppermute | solution.py:108
  1078.8 65.3 %collective-permute-start.11 = (f32[768,768]{1,0:T(8,128)}, f32[768,768]{1,0:T(8,128)}, u32[]{:S(2)}, u32[]{:S(2)}) collective-permute-start(f32[768,768]{1,0:T(8,128)} %fusion.124), channel_id=1, source_target_pairs={{0,1},{1,0},{2,3},{3,2},{4,5},{5,4},{6,7},{7,6}} | collective-permute-start | bytes 7077896 | tf_op jit(solution)/shard_map/ppermute | solution.py:108
  1078.9 65.7 %slice-start = ((s8[18874368]{0:T(1024)(128)(4,1)}), s8[4194304]{0:T(1024)(128)(4,1)S(1)}, s32[]{:S(2)}) async-start(s8[18874368]{0:T(1024)(128)(4,1)} %bitcast.111), calls=%async_computation.18 | async-start | bytes 8388608
  1078.9 65.7 %slice-start.1 = ((s8[18874368]{0:T(1024)(128)(4,1)}), s8[4194304]{0:T(1024)(128)(4,1)S(1)}, s32[]{:S(2)}) async-start(s8[18874368]{0:T(1024)(128)(4,1)} %bitcast.111), calls=%async_computation.19 | async-start | bytes 8388608
  1089.1 55.5 %slice-start.3 = ((s8[18874368]{0:T(1024)(128)(4,1)}), s8[4194304]{0:T(1024)(128)(4,1)S(1)}, s32[]{:S(2)}) async-start(s8[18874368]{0:T(1024)(128)(4,1)} %bitcast.111), calls=%async_computation.21 | async-start | bytes 8388608
  1089.1 55.5 %slice-start.4 = ((s8[18874368]{0:T(1024)(128)(4,1)}), s8[2097152]{0:T(1024)(128)(4,1)S(1)}, s32[]{:S(2)}) async-start(s8[18874368]{0:T(1024)(128)(4,1)} %bitcast.111), calls=%async_computation.22 | async-start | bytes 4194304
  1089.1 55.4 %collective-permute-start.10 = (f32[768,768]{1,0:T(8,128)}, f32[768,768]{1,0:T(8,128)}, u32[]{:S(2)}, u32[]{:S(2)}) collective-permute-start(f32[768,768]{1,0:T(8,128)} %fusion.130), channel_id=1, source_target_pairs={{0,1},{1,0},{2,3},{3,2},{4,5},{5,4},{6,7},{7,6}} | collective-permute-start | bytes 7077896 | tf_op jit(solution)/shard_map/ppermute | solution.py:108
  1089.5 106.2 %collective-permute-start.13 = (f32[768,768]{1,0:T(8,128)}, f32[768,768]{1,0:T(8,128)}, u32[]{:S(2)}, u32[]{:S(2)}) collective-permute-start(f32[768,768]{1,0:T(8,128)} %fusion.112), channel_id=1, source_target_pairs={{0,1},{1,0},{2,3},{3,2},{4,5},{5,4},{6,7},{7,6}} | collective-permute-start | bytes 7077896 | tf_op jit(solution)/shard_map/ppermute | solution.py:108
  1144.1 60.6 %collective-permute-start.12 = (f32[768,768]{1,0:T(8,128)}, f32[768,768]{1,0:T(8,128)}, u32[]{:S(2)}, u32[]{:S(2)}) collective-permute-start(f32[768,768]{1,0:T(8,128)} %fusion.122), channel_id=1, source_target_pairs={{0,1},{1,0},{2,3},{3,2},{4,5},{5,4},{6,7},{7,6}} | collective-permute-start | bytes 7077896 | tf_op jit(solution)/shard_map/ppermute | solution.py:108
  1144.5 81.5 %collective-permute-start.6 = (f32[1536,768]{1,0:T(8,128)S(1)}, f32[1536,768]{1,0:T(8,128)}, u32[]{:S(2)}, u32[]{:S(2)}) collective-permute-start(f32[1536,768]{1,0:T(8,128)S(1)} %fusion.126), channel_id=1, source_target_pairs={{0,1},{1,0},{2,3},{3,2},{4,5},{5,4},{6,7},{7,6}} | collective-permute-start | bytes 14155784 | tf_op jit(solution)/shard_map/ppermute | solution.py:108
  1195.8 37.9 %collective-permute-start.8 = (f32[768,1536]{1,0:T(8,128)}, f32[768,1536]{1,0:T(8,128)}, u32[]{:S(2)}, u32[]{:S(2)}) collective-permute-start(f32[768,1536]{1,0:T(8,128)} %fusion.128), channel_id=1, source_target_pairs={{0,1},{1,0},{2,3},{3,2},{4,5},{5,4},{6,7},{7,6}} | collective-permute-start | bytes 14155784 | tf_op jit(solution)/shard_map/ppermute | solution.py:108
  (28 other events, 706.1 us)
Sparse Core Ops, SparseCore 0:
  15.4 163.1 all-gather.23
  181.0 161.2 all-gather.9
  344.1 222.3 all-gather.13
  568.2 222.1 all-gather.11
  848.9 13.8 reduce-scatter.4
  875.8 13.8 reduce-scatter.6
  891.8 20.9 all-gather.15
  917.8 19.8 all-gather.17
  945.3 13.5 reduce-scatter.8
  961.0 14.9 reduce-scatter.10
  977.8 177.6 all-gather.19
  1157.2 173.9 all-gather.21
